TPU v7x, 256 devices: a whole 4x4x8 slice. The times are simulated.
256 devices in a mesh: batch: 16 (over y, x), field: 2 (over core), dim: 8 (over z).
Axes of the slice: x: 4, y: 4, z: 8, core: 2. Of those that a mesh axis runs over, the one named last changes fastest.
Arguments:
- features: bfloat16 [26, 128, 16384], P('field', 'dim', 'batch'), may hold values from -6 to 6
- cross_weight: bfloat16 [2, 26, 128, 26, 128], P(None, 'field', 'dim'), may hold values from -0.109375 to 0.109375
- cross_bias: float32 [2, 26, 128], P(None, 'field', 'dim'), may hold values from -3 to 3
- tower_weight: bfloat16 [1024, 26, 128], P(('field', 'dim')), may hold values from -0.109375 to 0.109375
- tower_bias: float32 [1024], P(('field', 'dim')), may hold values from -3 to 3
- query_weight: bfloat16 [1024, 128], P(('field', 'dim')), may hold values from -0.1875 to 0.1875
- user_vec: bfloat16 [16384, 128], P('batch'), may hold values from -6 to 6
- candidates: bfloat16 [4096, 128], P('batch'), may hold values from -6 to 6
- positive: int32 [16384], P('batch'), may hold values from 0 to 4095
Outputs:
- crossed: bfloat16 [26, 128, 16384], P('field', 'dim', 'batch')
- losses: float32 [16384], P('batch')
All inputs are finite; a program needn't handle non-finite values.
Results may differ from a plain program's by a relative error of at most 0.0049.
Values may be sent and summed in bfloat16 or wider, within the bound.
A program may use at most 64 MiB of HBM per device.

v0:
```python
import math
import jax
import jax.numpy as jnp
from jax import lax
from jax.sharding import Mesh
from jax.sharding import PartitionSpec as P

CROSS = 2
BATCH = ("batch_0", "batch_1")


def whole_of(x, axes, dim):
    if not axes:
        return x
    nearer = lax.all_gather(x, axes[-1], axis=dim, tiled=True)
    return whole_of(nearer, axes[:-1], dim)


def cut_along(x, dim, length):
    shape = x.shape
    pieces = x.reshape(*shape[:dim], length, shape[dim] // length, *shape[dim + 1 :])
    return jnp.moveaxis(pieces, dim, 0)


def summed_on_arrival(x, axis, dim):
    length = lax.axis_size(axis)
    pieces = lax.all_to_all(cut_along(x, dim, length), axis, 0, 0, tiled=True)
    return jnp.sum(pieces.astype(jnp.float32), axis=0)


def laid_out(pieces, dim):
    shape = list(pieces.shape[1:])
    shape[dim] *= pieces.shape[0]
    return jnp.moveaxis(pieces, 0, dim).reshape(shape)


def sent_to_all(x, axis):
    copies = jnp.broadcast_to(x, (lax.axis_size(axis), *x.shape))
    return lax.all_to_all(copies, axis, split_axis=0, concat_axis=0, tiled=True)


def gather_directly(x, axis, dim):
    return laid_out(sent_to_all(x, axis), dim)


def by_device(weights, field_count, dim_count):
    out_count, fields_all, entries_all = weights.shape
    shaped = weights.reshape(
        out_count, field_count, fields_all // field_count, dim_count, entries_all // dim_count
    )
    shaped = shaped.transpose(1, 3, 0, 2, 4)
    return shaped.reshape(
        field_count * dim_count, out_count, fields_all // field_count * (entries_all // dim_count)
    )


def row_adder(blocks, shards):
    return jnp.einsum("kib,koi->ob", shards, blocks, preferred_element_type=jnp.float32)


def cross_flat(current, blocks):
    field_local, entry_local, row_count = current.shape
    flattened = current.reshape(1, field_local * entry_local, row_count)
    return row_adder(blocks, lax.all_gather(flattened, ("field", "dim"), axis=0, tiled=True))


def next_layer(anchor, current, product, bias_vec):
    field_local, entry_local, row_count = current.shape
    gated = (product + bias_vec.reshape(field_local * entry_local, 1)).reshape(
        field_local, entry_local, row_count
    )
    return (anchor * gated + current.astype(jnp.float32)).astype(jnp.bfloat16)


def candidate_loss(query_vec, targets, candidates):
    score_scale = 1.0 / math.sqrt(query_vec.shape[1])
    row_count = query_vec.shape[0]
    running_max = jnp.full((row_count,), -1e30, jnp.float32)
    logits = (
        jnp.einsum(
            "be,ce->bc",
            query_vec,
            whole_of(candidates, BATCH, 0),
            preferred_element_type=jnp.float32,
        )
        * score_scale
    )
    labels = lax.broadcasted_iota(jnp.int32, logits.shape, 1)
    picked = jnp.sum(jnp.where(labels == targets[:, None], logits, 0.0), axis=1)
    new_max = jnp.maximum(running_max, jnp.max(logits, axis=1))
    running_sum = jnp.sum(jnp.exp(logits - new_max[:, None]), axis=1)
    best_score, exp_total, picked = (new_max, running_sum, picked)
    return best_score + jnp.log(exp_total) - picked


def body(
    features,
    cross_weight,
    cross_bias,
    tower_weight,
    tower_bias,
    query_weight,
    user_vec,
    candidates,
    positive,
):
    field_count = lax.axis_size("field")
    dim_count = lax.axis_size("dim")
    field_local, entry_local, row_count = features.shape
    column_count = field_local * entry_local
    anchor = features.astype(jnp.float32)
    current = features
    stacked = cross_weight.reshape(
        CROSS, column_count, cross_weight.shape[3], cross_weight.shape[4]
    )
    for level_idx in range(CROSS):
        blocks = by_device(stacked[level_idx], field_count, dim_count)
        product = cross_flat(current, blocks)
        current = next_layer(anchor, current, product, cross_bias[level_idx])
    tower_blocks = by_device(tower_weight, field_count, dim_count)
    flattened = current.reshape(1, column_count, row_count)
    tower_pre = row_adder(
        tower_blocks, lax.all_gather(flattened, ("field", "dim"), axis=0, tiled=True)
    )
    hidden = jax.nn.relu(tower_pre + tower_bias[:, None]).astype(jnp.bfloat16)
    partial_value = lax.dot_general(
        hidden, query_weight, (((0,), (0,)), ((), ())), preferred_element_type=jnp.float32
    )
    share_rows = row_count // (field_count * dim_count)
    member = lax.axis_index(("field", "dim"))
    query_part = summed_on_arrival(partial_value.astype(jnp.bfloat16), ("field", "dim"), 0)
    user_rows = lax.dynamic_slice_in_dim(user_vec, member * share_rows, share_rows, 0)
    targets = lax.dynamic_slice_in_dim(positive, member * share_rows, share_rows, 0)
    query_vec = (query_part + user_rows.astype(jnp.float32)).astype(jnp.bfloat16)
    part_loss = candidate_loss(query_vec, targets, candidates)
    losses = gather_directly(part_loss, ("field", "dim"), 0)
    return (current, losses)


def solution(mesh):
    torus = Mesh(
        mesh.devices.reshape(4, 4, mesh.shape["field"], mesh.shape["dim"]),
        ("batch_0", "batch_1", "field", "dim"),
    )
    in_specs = (
        P("field", "dim", BATCH),
        P(None, "field", "dim", None, None),
        P(None, "field", "dim"),
        P(("field", "dim"), None, None),
        P(("field", "dim")),
        P(("field", "dim"), None),
        P(BATCH, None),
        P(BATCH, None),
        P(BATCH),
    )
    out_specs = (P("field", "dim", BATCH), P(BATCH))
    return jax.shard_map(body, mesh=torus, in_specs=in_specs, out_specs=out_specs, check_vma=False)
```

profile of v0, /device:TPU:1, one launch (start us, length us, event | category | flops | bytes accessed | tf_op | source)
XLA Modules:
  0.0 219.8 jit_solution(14988092904554589448)
XLA Ops:
  7.2 0.7 all-gather.5.cloned.1.call-update
  8.0 2.2 %fusion.13 = (bf16[1,13,16,26,128]{4,2,3,1,0:T(8,128)(2,1)S(1)}, bf16[1,13,16,26,128]{4,2,3,1,0:T(8,128)(2,1)S(1)}) fusion(bf16[2,13,16,26,128]{4,2,3,1,0:T(8,128)(2,1)} %param.10), kind=kLoop, calls=%fused_computation.29 | loop fusion | bytes 5537792 | tf_op jit(solution)/shard_map/slice | solution.py:117
  10.2 0.2 copy.19
  10.4 8.7 %reshape_squeeze.8 = bf16[208,2,13,8,16]{4,3,0,2,1:T(8,128)(2,1)} reshape(bf16[1,13,16,26,128]{4,2,1,3,0:T(8,128)(2,1)S(1)} %copy.19) | data formatting | bytes 2768896 | tf_op jit(solution)/shard_map/reshape;squeeze | solution.py:48
  19.1 10.9 %copy.20 = bf16[2,8,208,13,16]{2,4,3,1,0:T(8,128)(2,1)S(1)} copy(bf16[2,8,208,13,16]{4,1,2,3,0:T(8,128)(2,1)} %bitcast.50) | data formatting | bytes 2768896 | tf_op jit(solution)/shard_map/transpose | solution.py:51
  30.1 0.1 add.51
  30.2 32.3 %all-gather.5.cloned.1.call-done = bf16[16,208,1024]{2,1,0:T(8,128)(2,1)} async-done(((bf16[1,208,1024]{2,1,0:T(8,128)(2,1)}), bf16[16,208,1024]{2,1,0:T(8,128)(2,1)}) %all-gather.5.cloned.1.call-update) | async-done | bytes 6815760 | tf_op jit(solution)/shard_map/all_gather | solution.py:64
  62.5 4.6 %fusion = f32[208,1024]{1,0:T(8,128)S(1)} fusion(bf16[16,208,208]{1,2,0:T(8,128)(2,1)S(1)} %bitcast.52, bf16[16,208,1024]{2,1,0:T(8,128)(2,1)} %all-gather.5.cloned.1.call-done, f32[208]{0:T(256)S(1)} %add.51), kind=kOutput, calls=%fused_computation.4 | convolution fusion | flops 1417887744 | bytes 9052992 | tf_op jit(solution)/shard_map/kib,koi->ob/dot_general | solution.py:58
  67.1 0.9 fusion.7
  68.0 0.0 all-gather.9.cloned.1.call-start
  68.1 0.2 copy.22
  68.3 8.7 %reshape_squeeze.9 = bf16[208,2,13,8,16]{4,3,0,2,1:T(8,128)(2,1)} reshape(bf16[1,13,16,26,128]{4,2,1,3,0:T(8,128)(2,1)S(1)} %copy.22) | data formatting | bytes 2768896 | tf_op jit(solution)/shard_map/reshape;squeeze | solution.py:48
  77.0 11.2 %copy.23 = bf16[2,8,208,13,16]{2,4,3,1,0:T(8,128)(2,1)S(1)} copy(bf16[2,8,208,13,16]{4,1,2,3,0:T(8,128)(2,1)} %bitcast.51) | data formatting | bytes 2768896 | tf_op jit(solution)/shard_map/transpose | solution.py:51
  88.2 0.1 add.55
  88.2 26.9 %all-gather.7.cloned.1.call-done = bf16[16,208,1024]{2,1,0:T(8,128)(2,1)} async-done(((bf16[1,208,1024]{2,1,0:T(8,128)(2,1)}), bf16[16,208,1024]{2,1,0:T(8,128)(2,1)}) %all-gather.7.cloned.1.call-update) | async-done | bytes 6815760 | tf_op jit(solution)/shard_map/all_gather | solution.py:64
  115.2 4.6 %fusion.1 = f32[1024,208]{0,1:T(8,128)S(1)} fusion(bf16[16,208,1024]{2,1,0:T(8,128)(2,1)} %all-gather.7.cloned.1.call-done, bf16[16,208,208]{1,2,0:T(8,128)(2,1)S(1)} %bitcast.58, f32[208]{0:T(256)S(1)} %add.55), kind=kOutput, calls=%fused_computation.5 | convolution fusion | flops 1417887744 | bytes 9052992 | tf_op jit(solution)/shard_map/kib,koi->ob/dot_general | solution.py:58
  119.9 1.0 fusion.6
  120.9 10.4 %all_gather.18 = bf16[1024,128]{1,0:T(8,128)(2,1)} all-gather(bf16[256,128]{1,0:T(8,128)(2,1)S(1)} %copy-done.4), channel_id=1, replica_groups=mesh['batch_0'=4,'batch_1'=4,'field'=2,'dim'=8] {'batch_1'}, dimensions={0}, use_global_device_ids=true | all-gather | bytes 327680 | tf_op jit(solution)/shard_map/all_gather | solution.py:15
  131.4 0.4 copy.25
  131.8 0.1 copy.26
  132.0 36.0 %all-gather.9.cloned.1.call-done = bf16[16,208,1024]{2,1,0:T(8,128)(2,1)} async-done(((bf16[1,208,1024]{2,1,0:T(8,128)(2,1)}), bf16[16,208,1024]{2,1,0:T(8,128)(2,1)}) %all-gather.9.cloned.1.call-update) | async-done | bytes 6815760 | tf_op jit(solution)/shard_map/all_gather | solution.py:123
  168.0 5.3 %convolution_convert_fusion = bf16[1024,128]{1,0:T(8,128)(2,1)} fusion(bf16[64,128]{1,0:T(8,128)(2,1)S(1)} %copy-done, bf16[16,208,1024]{2,1,0:T(8,128)(2,1)} %all-gather.9.cloned.1.call-done, bf16[16,64,208]{1,2,0:T(8,128)(2,1)S(1)} %bitcast.56, f32[64]{0:T(128)S(1)} %copy-done.6), kind=kOutput, calls=%fused_computation.6 | convolution fusion | flops 453312512 | bytes 7520512 | tf_op jit(solution)/shard_map/dot_general | solution.py:126
  173.3 4.6 %all-to-all-start = ((bf16[16,64,128]{2,1,0:T(8,128)(2,1)}), bf16[16,64,128]{2,1,0:T(8,128)(2,1)S(1)}, u32[]{:S(2)}, u32[]{:S(2)}) async-start(bf16[16,64,128]{2,1,0:T(8,128)(2,1)} %bitcast.16), calls=%async_computation | async-start | bytes 524288 | tf_op jit(solution)/shard_map/all_to_all | solution.py:27
  177.9 0.8 dynamic_slice.7
  178.6 8.9 %all-to-all-done = bf16[16,64,128]{2,1,0:T(8,128)(2,1)S(1)} async-done(((bf16[16,64,128]{2,1,0:T(8,128)(2,1)}), bf16[16,64,128]{2,1,0:T(8,128)(2,1)S(1)}, u32[]{:S(2)}, u32[]{:S(2)}) %all-to-all-start) | async-done | bytes 262176 | tf_op jit(solution)/shard_map/all_to_all | solution.py:27
  187.5 4.9 %all-gather.11.cloned.1.call-done = bf16[4096,128]{1,0:T(8,128)(2,1)} async-done(((bf16[1024,128]{1,0:T(8,128)(2,1)}), bf16[4096,128]{1,0:T(8,128)(2,1)}) %all-gather.11.cloned.1.call-update) | async-done | bytes 1048592 | tf_op jit(solution)/shard_map/all_gather | solution.py:15
  192.5 1.8 fusion.14
  194.3 0.5 exponential_reduce_fusion
  194.8 16.6 %all_to_all.11 = f32[16,1,64]{2,1,0:T(1,128)S(1)} all-to-all(f32[16,1,64]{2,1,0:T(1,128)S(1)} %broadcast_in_dim.15), channel_id=1, replica_groups=mesh['batch_0'=4,'batch_1'=4,'field'=2,'dim'=8] {'field','dim'}, dimensions={0} | all-to-all | bytes 8192 | tf_op jit(solution)/shard_map/all_to_all | solution.py:39
  211.4 0.5 broadcast.18
  211.9 0.7 reduce.7
  212.6 0.7 reshape.64
  (25 shorter events, 0.3 us)
Async XLA Ops:
  7.2 160.8 %copy-start = (bf16[64,128]{1,0:T(8,128)(2,1)S(1)}, bf16[64,128]{1,0:T(8,128)(2,1)}, u32[]{:S(2)}) copy-start(bf16[64,128]{1,0:T(8,128)(2,1)} %param.14) | copy-start | bytes 49156
  7.2 55.3 %all-gather.5.cloned.1.call-start = ((), (), s32[]{:S(2)}) async-start(), calls=%async_computation.2 | async-start | bytes 7241728 | tf_op jit(solution)/shard_map/all_gather | solution.py:64
  7.9 107.3 %all-gather.7.cloned.1.call-start = ((), (), s32[]{:S(2)}) async-start(), calls=%async_computation.3 | async-start | bytes 7241728 | tf_op jit(solution)/shard_map/all_gather | solution.py:64
  19.1 11.0 %copy-start.5 = (f32[2,13,16]{2,0,1:T(2,128)S(1)}, f32[2,13,16]{2,0,1:T(2,128)}, u32[]{:S(2)}) copy-start(f32[2,13,16]{2,0,1:T(2,128)} %param.11) | copy-start | bytes 4996
  62.5 4.6 %copy-start.1 = (bf16[13,16,1024]{2,1,0:T(8,128)(2,1)S(1)}, bf16[13,16,1024]{2,1,0:T(8,128)(2,1)}, u32[]{:S(2)}) copy-start(bf16[13,16,1024]{2,1,0:T(8,128)(2,1)} %param.9) | copy-start | bytes 1277956
  68.0 100.0 %all-gather.9.cloned.1.call-start = ((), (), s32[]{:S(2)}) async-start(), calls=%async_computation.4 | async-start | bytes 7241728 | tf_op jit(solution)/shard_map/all_gather | solution.py:123
  115.2 4.7 %copy-start.2 = (bf16[13,16,1024]{2,1,0:T(8,128)(2,1)S(1)}, bf16[13,16,1024]{2,1,0:T(8,128)(2,1)}, u32[]{:S(2)}) copy-start(bf16[13,16,1024]{2,1,0:T(8,128)(2,1)} %fusion.7) | copy-start | bytes 1277956
  115.2 5.7 %copy-start.4 = (bf16[256,128]{1,0:T(8,128)(2,1)S(1)}, bf16[256,128]{1,0:T(8,128)(2,1)}, u32[]{:S(2)}) copy-start(bf16[256,128]{1,0:T(8,128)(2,1)} %param.16) | copy-start | bytes 196612
  119.8 11.6 %copy-start.3 = (bf16[64,26,128]{2,0,1:T(8,128)(2,1)S(1)}, bf16[64,26,128]{2,0,1:T(8,128)(2,1)}, u32[]{:S(2)}) copy-start(bf16[64,26,128]{2,0,1:T(8,128)(2,1)} %param.12) | copy-start | bytes 1277956
  119.8 48.2 %copy-start.6 = (f32[64]{0:T(128)S(1)}, f32[64]{0:T(128)}, u32[]{:S(2)}) copy-start(f32[64]{0:T(128)} %param.13) | copy-start | bytes 772
  120.8 71.6 %all-gather.11.cloned.1.call-start = ((), (), s32[]{:S(2)}) async-start(), calls=%async_computation.5 | async-start | bytes 1310720 | tf_op jit(solution)/shard_map/all_gather | solution.py:15
  173.3 14.2 %all-to-all-start = ((bf16[16,64,128]{2,1,0:T(8,128)(2,1)}), bf16[16,64,128]{2,1,0:T(8,128)(2,1)S(1)}, u32[]{:S(2)}, u32[]{:S(2)}) async-start(bf16[16,64,128]{2,1,0:T(8,128)(2,1)} %bitcast.16), calls=%async_computation | async-start | bytes 524288 | tf_op jit(solution)/shard_map/all_to_all | solution.py:27
Sparse Core Ops, SparseCore 0:
  9.8 52.6 all-gather.4
  68.1 46.9 all-gather.6
  121.0 46.9 all-gather.8
  169.7 22.7 all-gather.10
where the time goes:
time: 220 us
  waiting for transfers between devices  110 us (50%)
  local copies, waits for them, and re-layouts  44.9 us (20%)
  blocking collectives  27 us (12%)
  matrix products  16.3 us (7%)
  between operations  13.9 us (6%)
  starting transfers between devices  4.74 us (2%)
  other arithmetic  3.03 us (1%)
    all_gather x2, waiting for transfers between devices, cross_flat(): lax.all_gather(flattened, ('field', 'dim'), axis=0, tiled=True)  59.2 us
    all_gather x1, waiting for transfers between devices, body(): lax.all_gather(flattened, ('field', 'dim'), axis=0, tiled=True)  36 us
    transpose x3, local copies, waits for them, and re-layouts, by_device(): shaped = shaped.transpose(1, 3, 0, 2, 4)  22.3 us
    another operation x2, local copies, waits for them, and re-layouts, by_device(): weights.reshape(out_count, field_count, fields_all // field_count, dim_co...  17.4 us
    all_to_all x1, blocking collectives, sent_to_all(): return lax.all_to_all(copies, axis, split_axis=0, concat_axis=0, tiled=True)  16.6 us
    all_gather x1, blocking collectives, whole_of(): nearer = lax.all_gather(x, axes[-1], axis=dim, tiled=True)  10.4 us
    dot_general x2, matrix products, row_adder(): jnp.einsum('kib,koi->ob', shards, blocks, preferred_element_type=jnp.floa...  9.24 us
    all_to_all x1, waiting for transfers between devices, summed_on_arrival(): pieces = lax.all_to_all(cut_along(x, dim, length), axis, 0, 0, tiled=True)  8.89 us
  transfers between devices with their start and end apart: 5, of which 5 were waited for; matrix products, arithmetic and copies ran while one was open for 22% of the time, Pallas kernels for 0%

commit v1 on v0

--- a/solution.py
+++ b/solution.py
@@ -1,3 +1,4 @@
+import functools
 import math
 import jax
 import jax.numpy as jnp
@@ -7,6 +8,35 @@
 
 CROSS = 2
 BATCH = ("batch_0", "batch_1")
+
+
+def search_cycles_by_axis(content, group_axis):
+    side_arr = jax.lax.psum(1, group_axis)
+    carry_out = jax.lax.axis_index(group_axis)
+    a_next, frame_out, long_array = (side_arr, carry_out, content.shape[0])
+    block_list = [dev * a_next if it == 0 else dev for it, dev in enumerate(content.shape)]
+    reached = jnp.zeros(block_list, content.dtype)
+    a_now = lax.dynamic_update_slice_in_dim(reached, content, frame_out * long_array, axis=0)
+    outer = outcome_arr = content
+    for rr in range(1, a_next // 2 + 1):
+        answer = list(map(lambda it: (it, (it + 1) % a_next), range(a_next)))
+        outer = jax.lax.ppermute(outer, group_axis, answer)
+        a_now = lax.dynamic_update_slice_in_dim(
+            a_now, outer, (frame_out - rr) % a_next * long_array, axis=0
+        )
+        if 2 * rr < a_next:
+            outcome_arr = jax.lax.ppermute(
+                outcome_arr,
+                group_axis,
+                list(map(lambda it: (it, (it - 1) % a_next), range(a_next))),
+            )
+            a_now = lax.dynamic_update_slice_in_dim(
+                a_now, outcome_arr, (frame_out + rr) % a_next * long_array, axis=0
+            )
+    return a_now
+
+
+apply_the_counts = functools.partial(search_cycles_by_axis, group_axis=("field", "dim"))
 
 
 def whole_of(x, axes, dim):
@@ -119,9 +149,7 @@
         current = next_layer(anchor, current, product, cross_bias[level_idx])
     tower_blocks = by_device(tower_weight, field_count, dim_count)
     flattened = current.reshape(1, column_count, row_count)
-    tower_pre = row_adder(
-        tower_blocks, lax.all_gather(flattened, ("field", "dim"), axis=0, tiled=True)
-    )
+    tower_pre = row_adder(tower_blocks, apply_the_counts(flattened))
     hidden = jax.nn.relu(tower_pre + tower_bias[:, None]).astype(jnp.bfloat16)
     partial_value = lax.dot_general(
         hidden, query_weight, (((0,), (0,)), ((), ())), preferred_element_type=jnp.float32

time: 220 us -> 275 us (1.25)
  starting transfers between devices: 4.74 us -> 29.2 us
  local copies, waits for them, and re-layouts: 44.9 us -> 66.4 us
  waiting for transfers between devices: 110 us -> 120 us
  blocking collectives: 27 us -> 23.3 us
    ppermute x0 -> x15, waiting for transfers between devices: none -> 52 us  [the longest x8 44.4 us: search_cycles_by_axis(): outer = jax.lax.ppermute(outer, group_axis, answer)]
    all_gather x1 -> x0, waiting for transfers between devices: 36 us -> none  [body(): lax.all_gather(flattened, ('field', 'dim'), axis=0, tiled=True)]
    ppermute x0 -> x15, starting transfers between devices: none -> 25.6 us  [the longest x7 23.9 us: search_cycles_by_axis(): jax.lax.ppermute(outcome_arr, group_axis, list(map(lambda it: (it, (it -...]
    dynamic_update_slice x0 -> x16, local copies, waits for them, and re-layouts: none -> 16.7 us  [the longest x8 8.37 us: search_cycles_by_axis(): lax.dynamic_update_slice_in_dim(a_now, outer, (frame_out - rr) % a_next *...]
    all_gather x1, waiting for transfers between devices: 4.93 us -> 0.03 us  [whole_of(): nearer = lax.all_gather(x, axes[-1], axis=dim, tiled=True)]
    all_to_all x1, blocking collectives: 16.6 us -> 12 us  [sent_to_all(): return lax.all_to_all(copies, axis, split_axis=0, concat_axis=0, tiled=True)]
    broadcast_in_dim x0 -> x1, local copies, waits for them, and re-layouts: none -> 3.71 us  [search_cycles_by_axis(): reached = jnp.zeros(block_list, content.dtype)]
  transfers between devices with their start and end apart: 5 -> 19, of which waited for: 5 -> 12; matrix products, arithmetic and copies ran while one was open for 22% -> 26% of each run, Pallas kernels for 0% -> 0%
where the time goes in v1:
time: 275 us; the launch traced here: 274 us
  waiting for transfers between devices  120 us (44%)
  local copies, waits for them, and re-layouts  66.4 us (24%)
  starting transfers between devices  29.2 us (11%)
  blocking collectives  23.3 us (8%)
  matrix products  16.4 us (6%)
  between operations  16.1 us (6%)
    all_gather x2, waiting for transfers between devices, cross_flat(): lax.all_gather(flattened, ('field', 'dim'), axis=0, tiled=True)  59.2 us
    ppermute x8, waiting for transfers between devices, search_cycles_by_axis(): outer = jax.lax.ppermute(outer, group_axis, answer)  44.4 us
    ppermute x7, starting transfers between devices, search_cycles_by_axis(): jax.lax.ppermute(outcome_arr, group_axis, list(map(lambda it: (it, (it -...  23.9 us
    transpose x3, local copies, waits for them, and re-layouts, by_device(): shaped = shaped.transpose(1, 3, 0, 2, 4)  22.2 us
    another operation x2, local copies, waits for them, and re-layouts, by_device(): weights.reshape(out_count, field_count, fields_all // field_count, dim_co...  17.4 us
    all_to_all x1, blocking collectives, sent_to_all(): return lax.all_to_all(copies, axis, split_axis=0, concat_axis=0, tiled=True)  12 us
    all_gather x1, blocking collectives, whole_of(): nearer = lax.all_gather(x, axes[-1], axis=dim, tiled=True)  11.3 us
    dot_general x2, matrix products, row_adder(): jnp.einsum('kib,koi->ob', shards, blocks, preferred_element_type=jnp.floa...  9.27 us
  transfers between devices with their start and end apart: 19, of which 12 were waited for; matrix products, arithmetic and copies ran while one was open for 26% of the time, Pallas kernels for 0%

profile of v1, /device:TPU:1, one launch (start us, length us, event | category | flops | bytes accessed | tf_op | source)
XLA Modules:
  0.0 273.7 jit_solution(653335440521482988)
XLA Ops:
  8.8 2.2 fusion.13
  11.3 8.7 %reshape_squeeze.8 = bf16[208,2,13,8,16]{4,3,0,2,1:T(8,128)(2,1)} reshape(bf16[1,13,16,26,128]{4,2,1,3,0:T(8,128)(2,1)S(1)} %copy.19) | data formatting | bytes 2768896 | tf_op jit(solution)/shard_map/reshape;squeeze | solution.py:78
  20.0 10.9 %copy.20 = bf16[2,8,208,13,16]{2,4,3,1,0:T(8,128)(2,1)S(1)} copy(bf16[2,8,208,13,16]{4,1,2,3,0:T(8,128)(2,1)} %bitcast.52) | data formatting | bytes 2768896 | tf_op jit(solution)/shard_map/transpose | solution.py:81
  31.1 32.3 %all-gather.4.cloned.1.call-done = bf16[16,208,1024]{2,1,0:T(8,128)(2,1)} async-done(((bf16[1,208,1024]{2,1,0:T(8,128)(2,1)}), bf16[16,208,1024]{2,1,0:T(8,128)(2,1)}) %all-gather.4.cloned.1.call-update) | async-done | bytes 6815760 | tf_op jit(solution)/shard_map/all_gather | solution.py:94
  63.3 4.6 %fusion = f32[208,1024]{1,0:T(8,128)S(1)} fusion(bf16[16,208,208]{1,2,0:T(8,128)(2,1)S(1)} %bitcast.54, bf16[16,208,1024]{2,1,0:T(8,128)(2,1)} %all-gather.4.cloned.1.call-done, f32[208]{0:T(256)S(1)} %add.175), kind=kOutput, calls=%fused_computation.4 | convolution fusion | flops 1417887744 | bytes 9052992 | tf_op jit(solution)/shard_map/kib,koi->ob/dot_general | solution.py:88
  69.2 8.7 %reshape_squeeze.9 = bf16[208,2,13,8,16]{4,3,0,2,1:T(8,128)(2,1)} reshape(bf16[1,13,16,26,128]{4,2,1,3,0:T(8,128)(2,1)S(1)} %copy.22) | data formatting | bytes 2768896 | tf_op jit(solution)/shard_map/reshape;squeeze | solution.py:78
  77.9 11.2 %copy.23 = bf16[2,8,208,13,16]{2,4,3,1,0:T(8,128)(2,1)S(1)} copy(bf16[2,8,208,13,16]{4,1,2,3,0:T(8,128)(2,1)} %bitcast.53) | data formatting | bytes 2768896 | tf_op jit(solution)/shard_map/transpose | solution.py:81
  89.1 26.9 %all-gather.6.cloned.1.call-done = bf16[16,208,1024]{2,1,0:T(8,128)(2,1)} async-done(((bf16[1,208,1024]{2,1,0:T(8,128)(2,1)}), bf16[16,208,1024]{2,1,0:T(8,128)(2,1)}) %all-gather.6.cloned.1.call-update) | async-done | bytes 6815760 | tf_op jit(solution)/shard_map/all_gather | solution.py:94
  116.0 4.6 %fusion.1 = f32[1024,208]{0,1:T(8,128)S(1)} fusion(bf16[16,208,1024]{2,1,0:T(8,128)(2,1)} %all-gather.6.cloned.1.call-done, bf16[16,208,208]{1,2,0:T(8,128)(2,1)S(1)} %bitcast.60, f32[208]{0:T(256)S(1)} %add.179), kind=kOutput, calls=%fused_computation.5 | convolution fusion | flops 1417887744 | bytes 9052992 | tf_op jit(solution)/shard_map/kib,koi->ob/dot_general | solution.py:88
  121.2 2.7 collective-permute-start.1
  123.9 10.0 %collective-permute-done = bf16[1,208,1024]{2,1,0:T(8,128)(2,1)S(1)} collective-permute-done((bf16[1,208,1024]{2,1,0:T(8,128)(2,1)S(1)}, bf16[1,208,1024]{2,1,0:T(8,128)(2,1)S(1)}, u32[]{:S(2)}, u32[]{:S(2)}) %collective-permute-start) | collective-permute-done | bytes 426016 | tf_op jit(solution)/shard_map/ppermute | solution.py:23
  133.9 2.9 %collective-permute-start.3 = (bf16[1,208,1024]{2,1,0:T(8,128)(2,1)S(1)}, bf16[1,208,1024]{2,1,0:T(8,128)(2,1)S(1)}, u32[]{:S(2)}, u32[]{:S(2)}) collective-permute-start(bf16[1,208,1024]{2,1,0:T(8,128)(2,1)S(1)} %collective-permute-done.1), channel_id=1, source_target_pairs={{0,15},{1,0},{2,1},{3,2},{4,3},{5,4},{6,5},{7,6},{8,7},{9,8},{10,9... | collective-permute-start | bytes 1277960 | tf_op jit(solution)/shard_map/ppermute | solution.py:28
  136.9 9.9 %collective-permute-done.2 = bf16[1,208,1024]{2,1,0:T(8,128)(2,1)S(1)} collective-permute-done((bf16[1,208,1024]{2,1,0:T(8,128)(2,1)S(1)}, bf16[1,208,1024]{2,1,0:T(8,128)(2,1)S(1)}, u32[]{:S(2)}, u32[]{:S(2)}) %collective-permute-start.2) | collective-permute-done | bytes 426016 | tf_op jit(solution)/shard_map/ppermute | solution.py:23
  146.8 3.0 %collective-permute-start.5 = (bf16[1,208,1024]{2,1,0:T(8,128)(2,1)S(1)}, bf16[1,208,1024]{2,1,0:T(8,128)(2,1)}, u32[]{:S(2)}, u32[]{:S(2)}) collective-permute-start(bf16[1,208,1024]{2,1,0:T(8,128)(2,1)S(1)} %collective-permute-done.3), channel_id=1, source_target_pairs={{0,15},{1,0},{2,1},{3,2},{4,3},{5,4},{6,5},{7,6},{8,7},{9,8},{10,9... | collective-permute-start | bytes 1277960 | tf_op jit(solution)/shard_map/ppermute | solution.py:28
  149.8 9.9 %collective-permute-done.4 = bf16[1,208,1024]{2,1,0:T(8,128)(2,1)S(1)} collective-permute-done((bf16[1,208,1024]{2,1,0:T(8,128)(2,1)S(1)}, bf16[1,208,1024]{2,1,0:T(8,128)(2,1)S(1)}, u32[]{:S(2)}, u32[]{:S(2)}) %collective-permute-start.4) | collective-permute-done | bytes 426016 | tf_op jit(solution)/shard_map/ppermute | solution.py:23
  159.7 3.0 %collective-permute-start.7 = (bf16[1,208,1024]{2,1,0:T(8,128)(2,1)}, bf16[1,208,1024]{2,1,0:T(8,128)(2,1)S(1)}, u32[]{:S(2)}, u32[]{:S(2)}) collective-permute-start(bf16[1,208,1024]{2,1,0:T(8,128)(2,1)} %collective-permute-done.5), channel_id=1, source_target_pairs={{0,15},{1,0},{2,1},{3,2},{4,3},{5,4},{6,5},{7,6},{8,7},{9,8},{10,9... | collective-permute-start | bytes 1277960 | tf_op jit(solution)/shard_map/ppermute | solution.py:28
  162.8 9.9 %collective-permute-done.6 = bf16[1,208,1024]{2,1,0:T(8,128)(2,1)S(1)} collective-permute-done((bf16[1,208,1024]{2,1,0:T(8,128)(2,1)S(1)}, bf16[1,208,1024]{2,1,0:T(8,128)(2,1)S(1)}, u32[]{:S(2)}, u32[]{:S(2)}) %collective-permute-start.6) | collective-permute-done | bytes 426016 | tf_op jit(solution)/shard_map/ppermute | solution.py:23
  172.7 11.3 %all_gather.14 = bf16[1024,128]{1,0:T(8,128)(2,1)} all-gather(bf16[256,128]{1,0:T(8,128)(2,1)S(1)} %copy-done.10), channel_id=1, replica_groups=mesh['batch_0'=4,'batch_1'=4,'field'=2,'dim'=8] {'batch_1'}, dimensions={0}, use_global_device_ids=true | all-gather | bytes 327680 | tf_op jit(solution)/shard_map/all_gather | solution.py:45
  185.9 3.7 %broadcast_in_dim.16 = bf16[16,208,1024]{2,1,0:T(8,128)(2,1)} broadcast(bf16[]{:T(256)} %constant.98.clone.1), dimensions={} | broadcast | bytes 6815746 | tf_op jit(solution)/shard_map/broadcast_in_dim | solution.py:18
  191.3 4.9 %collective-permute-start.9 = (bf16[1,208,1024]{2,1,0:T(8,128)(2,1)S(1)}, bf16[1,208,1024]{2,1,0:T(8,128)(2,1)S(1)}, u32[]{:S(2)}, u32[]{:S(2)}) collective-permute-start(bf16[1,208,1024]{2,1,0:T(8,128)(2,1)S(1)} %collective-permute-done.7), channel_id=1, source_target_pairs={{0,15},{1,0},{2,1},{3,2},{4,3},{5,4},{6,5},{7,6},{8,7},{9,8},{10,9... | collective-permute-start | bytes 1277960 | tf_op jit(solution)/shard_map/ppermute | solution.py:28
  201.4 2.0 collective-permute-done.9
  203.4 3.7 %collective-permute-start.11 = (bf16[1,208,1024]{2,1,0:T(8,128)(2,1)S(1)}, bf16[1,208,1024]{2,1,0:T(8,128)(2,1)S(1)}, u32[]{:S(2)}, u32[]{:S(2)}) collective-permute-start(bf16[1,208,1024]{2,1,0:T(8,128)(2,1)S(1)} %collective-permute-done.9), channel_id=1, source_target_pairs={{0,15},{1,0},{2,1},{3,2},{4,3},{5,4},{6,5},{7,6},{8,7},{9,8},{10,9... | collective-permute-start | bytes 1277960 | tf_op jit(solution)/shard_map/ppermute | solution.py:28
  210.5 1.8 constant_dynamic-update-slice_fusion.6
  212.3 2.3 collective-permute-done.11
  214.7 3.7 %collective-permute-start.13 = (bf16[1,208,1024]{2,1,0:T(8,128)(2,1)S(1)}, bf16[1,208,1024]{2,1,0:T(8,128)(2,1)S(1)}, u32[]{:S(2)}, u32[]{:S(2)}) collective-permute-start(bf16[1,208,1024]{2,1,0:T(8,128)(2,1)S(1)} %collective-permute-done.11), channel_id=1, source_target_pairs={{0,15},{1,0},{2,1},{3,2},{4,3},{5,4},{6,5},{7,6},{8,7},{9,8},{10,9... | collective-permute-start | bytes 1277960 | tf_op jit(solution)/shard_map/ppermute | solution.py:28
  223.0 3.2 %collective-permute-done.13 = bf16[1,208,1024]{2,1,0:T(8,128)(2,1)S(1)} collective-permute-done((bf16[1,208,1024]{2,1,0:T(8,128)(2,1)S(1)}, bf16[1,208,1024]{2,1,0:T(8,128)(2,1)S(1)}, u32[]{:S(2)}, u32[]{:S(2)}) %collective-permute-start.13) | collective-permute-done | bytes 426016 | tf_op jit(solution)/shard_map/ppermute | solution.py:28
  227.0 4.5 %collective-permute-done.14 = bf16[1,208,1024]{2,1,0:T(8,128)(2,1)S(1)} collective-permute-done((bf16[1,208,1024]{2,1,0:T(8,128)(2,1)S(1)}, bf16[1,208,1024]{2,1,0:T(8,128)(2,1)S(1)}, u32[]{:S(2)}, u32[]{:S(2)}) %collective-permute-start.14) | collective-permute-done | bytes 426016 | tf_op jit(solution)/shard_map/ppermute | solution.py:23
  232.3 5.3 %convolution_convert_fusion = bf16[1024,128]{1,0:T(8,128)(2,1)} fusion(bf16[64,128]{1,0:T(8,128)(2,1)S(1)} %copy-done, bf16[16,208,1024]{2,1,0:T(8,128)(2,1)} %constant_dynamic-update-slice_fusion, bf16[16,64,208]{1,2,0:T(8,128)(2,1)S(1)} %bitcast.58, f32[64]{0:T(128)S(1)} %copy-done.12), kind=kOutput, calls=%fused_computation.6 | convolution fusion | flops 453312512 | bytes 7520512 | tf_op jit(solution)/shard_map/dot_general | solution.py:154
  237.6 3.4 %all-to-all-start = ((bf16[16,64,128]{2,1,0:T(8,128)(2,1)}), bf16[16,64,128]{2,1,0:T(8,128)(2,1)S(1)}, u32[]{:S(2)}, u32[]{:S(2)}) async-start(bf16[16,64,128]{2,1,0:T(8,128)(2,1)} %bitcast.16), calls=%async_computation | async-start | bytes 524288 | tf_op jit(solution)/shard_map/all_to_all | solution.py:57
  241.8 8.2 %all-to-all-done = bf16[16,64,128]{2,1,0:T(8,128)(2,1)S(1)} async-done(((bf16[16,64,128]{2,1,0:T(8,128)(2,1)}), bf16[16,64,128]{2,1,0:T(8,128)(2,1)S(1)}, u32[]{:S(2)}, u32[]{:S(2)}) %all-to-all-start) | async-done | bytes 262176 | tf_op jit(solution)/shard_map/all_to_all | solution.py:57
  250.1 1.8 fusion.14
  252.4 12.0 %all_to_all.11 = f32[16,1,64]{2,1,0:T(1,128)S(1)} all-to-all(f32[16,1,64]{2,1,0:T(1,128)S(1)} %broadcast_in_dim.19), channel_id=1, replica_groups=mesh['batch_0'=4,'batch_1'=4,'field'=2,'dim'=8] {'field','dim'}, dimensions={0} | all-to-all | bytes 8192 | tf_op jit(solution)/shard_map/all_to_all | solution.py:69
  (81 shorter events, 24.1 us)
Async XLA Ops:
  8.0 224.3 %copy-start = (bf16[64,128]{1,0:T(8,128)(2,1)S(1)}, bf16[64,128]{1,0:T(8,128)(2,1)}, u32[]{:S(2)}) copy-start(bf16[64,128]{1,0:T(8,128)(2,1)} %param.14) | copy-start | bytes 49156
  8.0 55.3 %all-gather.4.cloned.1.call-start = ((), (), s32[]{:S(2)}) async-start(), calls=%async_computation.2 | async-start | bytes 7241728 | tf_op jit(solution)/shard_map/all_gather | solution.py:94
  8.7 107.3 %all-gather.6.cloned.1.call-start = ((), (), s32[]{:S(2)}) async-start(), calls=%async_computation.3 | async-start | bytes 7241728 | tf_op jit(solution)/shard_map/all_gather | solution.py:94
  20.0 11.0 %copy-start.11 = (f32[2,13,16]{2,0,1:T(2,128)S(1)}, f32[2,13,16]{2,0,1:T(2,128)}, u32[]{:S(2)}) copy-start(f32[2,13,16]{2,0,1:T(2,128)} %param.11) | copy-start | bytes 4996
  63.3 4.6 %copy-start.1 = (bf16[13,16,1024]{2,1,0:T(8,128)(2,1)S(1)}, bf16[13,16,1024]{2,1,0:T(8,128)(2,1)}, u32[]{:S(2)}) copy-start(bf16[13,16,1024]{2,1,0:T(8,128)(2,1)} %param.9) | copy-start | bytes 1277956
  68.9 181.2 %all-gather.8.cloned.1.call-start = ((), (), s32[]{:S(2)}) async-start(), calls=%async_computation.4 | async-start | bytes 1310720 | tf_op jit(solution)/shard_map/all_gather | solution.py:45
  89.0 31.7 %copy-start.2 = (bf16[13,16,1024]{2,1,0:T(8,128)(2,1)S(1)}, bf16[13,16,1024]{2,1,0:T(8,128)(2,1)}, u32[]{:S(2)}) copy-start(bf16[13,16,1024]{2,1,0:T(8,128)(2,1)} %fusion.7) | copy-start | bytes 1277956
  116.0 56.6 %copy-start.10 = (bf16[256,128]{1,0:T(8,128)(2,1)S(1)}, bf16[256,128]{1,0:T(8,128)(2,1)}, u32[]{:S(2)}) copy-start(bf16[256,128]{1,0:T(8,128)(2,1)} %param.16) | copy-start | bytes 196612
  120.9 76.9 %copy-start.3 = (bf16[13,16,1024]{2,1,0:T(8,128)(2,1)}, bf16[13,16,1024]{2,1,0:T(8,128)(2,1)S(1)}, u32[]{:S(2)}) copy-start(bf16[13,16,1024]{2,1,0:T(8,128)(2,1)S(1)} %fusion.6) | copy-start | bytes 1277956
  120.9 13.0 %collective-permute-start = (bf16[1,208,1024]{2,1,0:T(8,128)(2,1)S(1)}, bf16[1,208,1024]{2,1,0:T(8,128)(2,1)S(1)}, u32[]{:S(2)}, u32[]{:S(2)}) collective-permute-start(bf16[1,208,1024]{2,1,0:T(8,128)(2,1)S(1)} %bitcast.61), channel_id=1, source_target_pairs={{0,1},{1,2},{2,3},{3,4},{4,5},{5,6},{6,7},{7,8},{8,9},{9,10},{10,1... | collective-permute-start | bytes 1277960 | tf_op jit(solution)/shard_map/ppermute | solution.py:23
  121.2 12.7 %collective-permute-start.1 = (bf16[1,208,1024]{2,1,0:T(8,128)(2,1)S(1)}, bf16[1,208,1024]{2,1,0:T(8,128)(2,1)S(1)}, u32[]{:S(2)}, u32[]{:S(2)}) collective-permute-start(bf16[1,208,1024]{2,1,0:T(8,128)(2,1)S(1)} %bitcast.62), channel_id=1, source_target_pairs={{0,15},{1,0},{2,1},{3,2},{4,3},{5,4},{6,5},{7,6},{8,7},{9,8},{10,9... | collective-permute-start | bytes 1277960 | tf_op jit(solution)/shard_map/ppermute | solution.py:28
  133.9 3.0 %copy-start.8 = (bf16[1,208,1024]{2,1,0:T(8,128)(2,1)}, bf16[1,208,1024]{2,1,0:T(8,128)(2,1)S(1)}, u32[]{:S(2)}) copy-start(bf16[1,208,1024]{2,1,0:T(8,128)(2,1)S(1)} %collective-permute-done) | copy-start | bytes 1277956
  133.9 12.9 %collective-permute-start.2 = (bf16[1,208,1024]{2,1,0:T(8,128)(2,1)S(1)}, bf16[1,208,1024]{2,1,0:T(8,128)(2,1)S(1)}, u32[]{:S(2)}, u32[]{:S(2)}) collective-permute-start(bf16[1,208,1024]{2,1,0:T(8,128)(2,1)S(1)} %collective-permute-done), channel_id=1, source_target_pairs={{0,1},{1,2},{2,3},{3,4},{4,5},{5,6},{6,7},{7,8},{8,9},{9,10},{10,1... | collective-permute-start | bytes 1277960 | tf_op jit(solution)/shard_map/ppermute | solution.py:23
  133.9 15.9 %copy-start.5 = (bf16[1,208,1024]{2,1,0:T(8,128)(2,1)}, bf16[1,208,1024]{2,1,0:T(8,128)(2,1)S(1)}, u32[]{:S(2)}) copy-start(bf16[1,208,1024]{2,1,0:T(8,128)(2,1)S(1)} %collective-permute-done.1) | copy-start | bytes 1277956
  133.9 12.9 %collective-permute-start.3 = (bf16[1,208,1024]{2,1,0:T(8,128)(2,1)S(1)}, bf16[1,208,1024]{2,1,0:T(8,128)(2,1)S(1)}, u32[]{:S(2)}, u32[]{:S(2)}) collective-permute-start(bf16[1,208,1024]{2,1,0:T(8,128)(2,1)S(1)} %collective-permute-done.1), channel_id=1, source_target_pairs={{0,15},{1,0},{2,1},{3,2},{4,3},{5,4},{6,5},{7,6},{8,7},{9,8},{10,9... | collective-permute-start | bytes 1277960 | tf_op jit(solution)/shard_map/ppermute | solution.py:28
  146.8 12.9 %collective-permute-start.4 = (bf16[1,208,1024]{2,1,0:T(8,128)(2,1)S(1)}, bf16[1,208,1024]{2,1,0:T(8,128)(2,1)S(1)}, u32[]{:S(2)}, u32[]{:S(2)}) collective-permute-start(bf16[1,208,1024]{2,1,0:T(8,128)(2,1)S(1)} %collective-permute-done.2), channel_id=1, source_target_pairs={{0,1},{1,2},{2,3},{3,4},{4,5},{5,6},{6,7},{7,8},{8,9},{9,10},{10,1... | collective-permute-start | bytes 1277960 | tf_op jit(solution)/shard_map/ppermute | solution.py:23
  146.8 25.8 %copy-start.4 = (bf16[1,208,1024]{2,1,0:T(8,128)(2,1)}, bf16[1,208,1024]{2,1,0:T(8,128)(2,1)S(1)}, u32[]{:S(2)}) copy-start(bf16[1,208,1024]{2,1,0:T(8,128)(2,1)S(1)} %collective-permute-done.3) | copy-start | bytes 1277956
  146.8 12.9 %collective-permute-start.5 = (bf16[1,208,1024]{2,1,0:T(8,128)(2,1)S(1)}, bf16[1,208,1024]{2,1,0:T(8,128)(2,1)}, u32[]{:S(2)}, u32[]{:S(2)}) collective-permute-start(bf16[1,208,1024]{2,1,0:T(8,128)(2,1)S(1)} %collective-permute-done.3), channel_id=1, source_target_pairs={{0,15},{1,0},{2,1},{3,2},{4,3},{5,4},{6,5},{7,6},{8,7},{9,8},{10,9... | collective-permute-start | bytes 1277960 | tf_op jit(solution)/shard_map/ppermute | solution.py:28
  159.7 12.9 %copy-start.7 = (bf16[1,208,1024]{2,1,0:T(8,128)(2,1)}, bf16[1,208,1024]{2,1,0:T(8,128)(2,1)S(1)}, u32[]{:S(2)}) copy-start(bf16[1,208,1024]{2,1,0:T(8,128)(2,1)S(1)} %collective-permute-done.4) | copy-start | bytes 1277956
  159.7 12.9 %collective-permute-start.6 = (bf16[1,208,1024]{2,1,0:T(8,128)(2,1)S(1)}, bf16[1,208,1024]{2,1,0:T(8,128)(2,1)S(1)}, u32[]{:S(2)}, u32[]{:S(2)}) collective-permute-start(bf16[1,208,1024]{2,1,0:T(8,128)(2,1)S(1)} %collective-permute-done.4), channel_id=1, source_target_pairs={{0,1},{1,2},{2,3},{3,4},{4,5},{5,6},{6,7},{7,8},{8,9},{9,10},{10,1... | collective-permute-start | bytes 1277960 | tf_op jit(solution)/shard_map/ppermute | solution.py:23
  159.7 31.5 %collective-permute-start.7 = (bf16[1,208,1024]{2,1,0:T(8,128)(2,1)}, bf16[1,208,1024]{2,1,0:T(8,128)(2,1)S(1)}, u32[]{:S(2)}, u32[]{:S(2)}) collective-permute-start(bf16[1,208,1024]{2,1,0:T(8,128)(2,1)} %collective-permute-done.5), channel_id=1, source_target_pairs={{0,15},{1,0},{2,1},{3,2},{4,3},{5,4},{6,5},{7,6},{8,7},{9,8},{10,9... | collective-permute-start | bytes 1277960 | tf_op jit(solution)/shard_map/ppermute | solution.py:28
  172.6 24.3 %collective-permute-start.8 = (bf16[1,208,1024]{2,1,0:T(8,128)(2,1)S(1)}, bf16[1,208,1024]{2,1,0:T(8,128)(2,1)}, u32[]{:S(2)}, u32[]{:S(2)}) collective-permute-start(bf16[1,208,1024]{2,1,0:T(8,128)(2,1)S(1)} %collective-permute-done.6), channel_id=1, source_target_pairs={{0,1},{1,2},{2,3},{3,4},{4,5},{5,6},{6,7},{7,8},{8,9},{9,10},{10,1... | collective-permute-start | bytes 1277960 | tf_op jit(solution)/shard_map/ppermute | solution.py:23
  185.8 4.6 %copy-start.9 = (bf16[1,208,1024]{2,1,0:T(8,128)(2,1)S(1)}, bf16[1,208,1024]{2,1,0:T(8,128)(2,1)}, u32[]{:S(2)}) copy-start(bf16[1,208,1024]{2,1,0:T(8,128)(2,1)} %copy-done.8) | copy-start | bytes 1277956
  185.8 10.4 %copy-start.6 = (bf16[1,208,1024]{2,1,0:T(8,128)(2,1)S(1)}, bf16[1,208,1024]{2,1,0:T(8,128)(2,1)}, u32[]{:S(2)}) copy-start(bf16[1,208,1024]{2,1,0:T(8,128)(2,1)} %copy-done.5) | copy-start | bytes 1277956
  189.6 42.7 %copy-start.12 = (f32[64]{0:T(128)S(1)}, f32[64]{0:T(128)}, u32[]{:S(2)}) copy-start(f32[64]{0:T(128)} %param.13) | copy-start | bytes 772
  191.3 12.1 %collective-permute-start.9 = (bf16[1,208,1024]{2,1,0:T(8,128)(2,1)S(1)}, bf16[1,208,1024]{2,1,0:T(8,128)(2,1)S(1)}, u32[]{:S(2)}, u32[]{:S(2)}) collective-permute-start(bf16[1,208,1024]{2,1,0:T(8,128)(2,1)S(1)} %collective-permute-done.7), channel_id=1, source_target_pairs={{0,15},{1,0},{2,1},{3,2},{4,3},{5,4},{6,5},{7,6},{8,7},{9,8},{10,9... | collective-permute-start | bytes 1277960 | tf_op jit(solution)/shard_map/ppermute | solution.py:28
  197.0 11.9 %collective-permute-start.10 = (bf16[1,208,1024]{2,1,0:T(8,128)(2,1)}, bf16[1,208,1024]{2,1,0:T(8,128)(2,1)S(1)}, u32[]{:S(2)}, u32[]{:S(2)}) collective-permute-start(bf16[1,208,1024]{2,1,0:T(8,128)(2,1)} %collective-permute-done.8), channel_id=1, source_target_pairs={{0,1},{1,2},{2,3},{3,4},{4,5},{5,6},{6,7},{7,8},{8,9},{9,10},{10,1... | collective-permute-start | bytes 1277960 | tf_op jit(solution)/shard_map/ppermute | solution.py:23
  203.4 11.3 %collective-permute-start.11 = (bf16[1,208,1024]{2,1,0:T(8,128)(2,1)S(1)}, bf16[1,208,1024]{2,1,0:T(8,128)(2,1)S(1)}, u32[]{:S(2)}, u32[]{:S(2)}) collective-permute-start(bf16[1,208,1024]{2,1,0:T(8,128)(2,1)S(1)} %collective-permute-done.9), channel_id=1, source_target_pairs={{0,15},{1,0},{2,1},{3,2},{4,3},{5,4},{6,5},{7,6},{8,7},{9,8},{10,9... | collective-permute-start | bytes 1277960 | tf_op jit(solution)/shard_map/ppermute | solution.py:28
  208.9 10.4 %collective-permute-start.12 = (bf16[1,208,1024]{2,1,0:T(8,128)(2,1)S(1)}, bf16[1,208,1024]{2,1,0:T(8,128)(2,1)S(1)}, u32[]{:S(2)}, u32[]{:S(2)}) collective-permute-start(bf16[1,208,1024]{2,1,0:T(8,128)(2,1)S(1)} %collective-permute-done.10), channel_id=1, source_target_pairs={{0,1},{1,2},{2,3},{3,4},{4,5},{5,6},{6,7},{7,8},{8,9},{9,10},{10,1... | collective-permute-start | bytes 1277960 | tf_op jit(solution)/shard_map/ppermute | solution.py:23
  214.7 11.6 %collective-permute-start.13 = (bf16[1,208,1024]{2,1,0:T(8,128)(2,1)S(1)}, bf16[1,208,1024]{2,1,0:T(8,128)(2,1)S(1)}, u32[]{:S(2)}, u32[]{:S(2)}) collective-permute-start(bf16[1,208,1024]{2,1,0:T(8,128)(2,1)S(1)} %collective-permute-done.11), channel_id=1, source_target_pairs={{0,15},{1,0},{2,1},{3,2},{4,3},{5,4},{6,5},{7,6},{8,7},{9,8},{10,9... | collective-permute-start | bytes 1277960 | tf_op jit(solution)/shard_map/ppermute | solution.py:28
  219.3 12.3 %collective-permute-start.14 = (bf16[1,208,1024]{2,1,0:T(8,128)(2,1)S(1)}, bf16[1,208,1024]{2,1,0:T(8,128)(2,1)S(1)}, u32[]{:S(2)}, u32[]{:S(2)}) collective-permute-start(bf16[1,208,1024]{2,1,0:T(8,128)(2,1)S(1)} %collective-permute-done.12), channel_id=1, source_target_pairs={{0,1},{1,2},{2,3},{3,4},{4,5},{5,6},{6,7},{7,8},{8,9},{9,10},{10,1... | collective-permute-start | bytes 1277960 | tf_op jit(solution)/shard_map/ppermute | solution.py:23
  237.6 12.4 %all-to-all-start = ((bf16[16,64,128]{2,1,0:T(8,128)(2,1)}), bf16[16,64,128]{2,1,0:T(8,128)(2,1)S(1)}, u32[]{:S(2)}, u32[]{:S(2)}) async-start(bf16[16,64,128]{2,1,0:T(8,128)(2,1)} %bitcast.16), calls=%async_computation | async-start | bytes 524288 | tf_op jit(solution)/shard_map/all_to_all | solution.py:57
Sparse Core Ops, SparseCore 0:
  10.6 52.6 all-gather.3
  69.0 46.9 all-gather.5
Sparse Core Ops, SparseCore 1:
  184.1 24.1 all-gather.7
